TPU v7x, 256 devices: a whole 4x4x8 slice. The times are simulated.
256 devices in a mesh: field: 32 (over z, x), vrow: 2 (over core), vcol: 4 (over y).
Axes of the slice: x: 4, y: 4, z: 8, core: 2. Of those that a mesh axis runs over, the one named last changes fastest.
Arguments:
- blocks: bfloat16 [1024, 192, 2, 256], P(('vrow', 'vcol'), 'field'), may hold values from 0 to 1
- block_ids: int32 [8, 32, 6], P(('vrow', 'vcol'), 'field'), may hold values from 0 to 11, as said below
- block_counts: int32 [8, 32], P(('vrow', 'vcol'), 'field'), may hold values from 1 to 6, as said below
Outputs:
- tables: float32 [1024, 2, 2, 4, 2, 128], P(('vrow', 'field'), None, None, 'vcol')
Inputs may be any that keep to these rules, and one draw needn't show every extreme that they name: `block_ids`: within each row of the last dimension the entries are distinct. `block_counts`: 6 is reached in every draw.
All inputs are finite; a program needn't handle non-finite values.
Results may differ from a plain program's by a relative error of at most 0.0003.
Values may be sent and summed in bfloat16 or wider, within the bound.
No kernel may reach another device: no remote copies, remote signals or barrier semaphores. Data moves between devices by JAX's collectives and lax.ppermute only.
A program may use at most 64 MiB of HBM per device.

v0:
```python
import math
import jax
import jax.numpy as jnp
from jax import lax
from jax.sharding import PartitionSpec as P

SBLK = 12
BLOCK = 256


def side_by_side(arrays, axis, dim, along):
    widths = [math.prod(a.shape[along:]) for a in arrays]
    both = jnp.concatenate(
        [a.reshape(*a.shape[:along], w) for a, w in zip(arrays, widths)], axis=along
    )
    out = lax.all_gather(both, axis, axis=dim, tiled=True)
    parts = jnp.split(out, [sum(widths[:k]) for k in range(1, len(widths))], axis=along)
    return tuple((b.reshape(*out.shape[:along], *a.shape[along:]) for a, b in zip(arrays, parts)))


def split_up(array, dim, length):
    dims = array.shape
    parts = array.reshape(*dims[:dim], length, dims[dim] // length, *dims[dim + 1 :])
    return jnp.moveaxis(parts, dim, 0)


def sent_and_summed(array, axis, dim):
    length = lax.axis_size(axis)
    parts = lax.all_to_all(split_up(array, dim, length), axis, 0, 0, tiled=True)
    return jnp.sum(parts, axis=0)


def expand(blocks, block_ids, block_counts):
    shards = block_ids.shape[0]
    occ = block_ids.shape[-1]
    shaped = blocks.reshape(shards, blocks.shape[0] // shards, occ, 2, blocks.shape[-1])
    slots = jnp.arange(occ, dtype=jnp.int32)
    live = slots[None, :] < block_counts[:, 0][:, None]
    onehot = (block_ids[:, 0, :, None] == jnp.arange(SBLK, dtype=jnp.int32)[None, None, :]) & live[
        ..., None
    ]
    dense = jnp.einsum(
        "sok,svocx->svkcx", onehot.astype(jnp.bfloat16), shaped, preferred_element_type=jnp.float32
    )
    return dense.astype(jnp.bfloat16).reshape(blocks.shape[0], SBLK, 2, blocks.shape[-1])


def on_device(blocks, block_ids, block_counts):
    row_data, row_ids, row_counts = (
        lax.all_gather(blocks, "vcol", axis=0, tiled=True),
        *side_by_side((block_ids, block_counts), "vcol", 0, 2),
    )
    rows = expand(row_data, row_ids, row_counts)
    col_data, col_ids, col_counts = (
        lax.all_gather(blocks, "vrow", axis=0, tiled=True),
        *side_by_side((block_ids, block_counts), "vrow", 0, 2),
    )
    columns = expand(col_data, col_ids, col_counts)
    groups = lax.axis_size("vrow")
    columns = columns.reshape(groups, columns.shape[0] // groups, SBLK, 2, columns.shape[-1])
    fields = lax.axis_size("field")
    term = jnp.einsum("ikcx,rjkdx->icrdj", rows, columns, preferred_element_type=jnp.float32)
    summed = sent_and_summed(term[:, :, :, None], "field", 0)
    return summed / (fields * SBLK * BLOCK)


def solution(mesh):
    placed = (
        P(("vrow", "vcol"), "field", None, None),
        P(("vrow", "vcol"), "field", None),
        P(("vrow", "vcol"), "field"),
    )
    return jax.shard_map(
        on_device,
        mesh=mesh,
        in_specs=placed,
        out_specs=P(("vrow", "field"), None, None, "vcol", None, None),
        check_vma=False,
    )
```

profile of v0, /device:TPU:2, one launch (start us, length us, event | category | flops | bytes accessed | tf_op | source)
XLA Modules:
  0.0 164.3 jit_solution(4973293619530026705)
XLA Ops:
  6.5 0.0 all-gather.3.cloned.1.call-start
  6.5 0.7 all-gather.3.cloned.1.call-update
  7.3 0.0 all-gather.5.cloned.1.call-start
  7.3 0.7 all-gather.5.cloned.1.call-update
  8.7 0.7 pad_add_fusion
  9.4 1.8 %all_gather.12 = s32[2,1,7]{2,1,0:T(1,128)S(1)} all-gather(s32[1,1,7]{2,1,0:T(1,128)S(1)} %pad_add_fusion), channel_id=1, replica_groups=mesh['field'=32,'vrow'=2,'vcol'=4] {'vrow'}, dimensions={0}, use_global_device_ids=true | all-gather | bytes 84 | tf_op jit(solution)/shard_map/all_gather | solution.py:16
  11.2 10.0 %all_gather.14 = s32[4,1,7]{2,1,0:T(1,128)S(1)} all-gather(s32[1,1,7]{2,1,0:T(1,128)S(1)} %pad_add_fusion), channel_id=1, replica_groups=mesh['field'=32,'vrow'=2,'vcol'=4] {'vcol'}, dimensions={0}, use_global_device_ids=true | all-gather | bytes 140 | tf_op jit(solution)/shard_map/all_gather | solution.py:16
  21.1 0.2 slice_reduce_fusion.1
  21.3 0.2 slice_reduce_fusion
  21.6 0.1 iota_compare_fusion.2
  21.6 0.1 iota_compare_fusion.3
  21.7 5.5 %all-gather.3.cloned.1.call-done = bf16[256,6,2,256]{3,2,1,0:T(2,128)(2,1)} async-done(((bf16[128,6,2,256]{3,2,1,0:T(2,128)(2,1)}), bf16[256,6,2,256]{3,2,1,0:T(2,128)(2,1)}) %all-gather.3.cloned.1.call-update) | async-done | bytes 1572880 | tf_op jit(solution)/shard_map/all_gather | solution.py:55
  27.2 1.9 %copy.9 = bf16[256,6,2,256]{3,1,2,0:T(8,128)(2,1)S(1)} copy(bf16[256,6,2,256]{3,2,1,0:T(2,128)(2,1)} %all-gather.3.cloned.1.call-done) | data formatting | bytes 3145728 | tf_op jit(solution)/shard_map/all_gather | solution.py:55
  29.1 3.1 %convert_bitcast_fusion = bf16[2,128,12,2,256,1]{4,2,3,1,0,5:T(8,128)(2,1)} fusion(bf16[2,128,6,2,256]{4,2,3,1,0:T(8,128)(2,1)S(1)} %bitcast.39, s32[2,6]{1,0:T(2,128)S(1)} %bitcast.42, pred[2,6]{1,0:T(4,128)(4,1)S(1)} %iota_compare_fusion.3), kind=kOutput, calls=%fused_computation.3 | convolution fusion | flops 20447520 | bytes 4718652 | tf_op jit(solution)/shard_map/sok,svocx->svkcx/dot_general | solution.py:42
  32.2 40.3 %all-gather.5.cloned.1.call-done = bf16[512,6,2,256]{3,2,1,0:T(2,128)(2,1)} async-done(((bf16[128,6,2,256]{3,2,1,0:T(2,128)(2,1)}), bf16[512,6,2,256]{3,2,1,0:T(2,128)(2,1)}) %all-gather.5.cloned.1.call-update) | async-done | bytes 3145744 | tf_op jit(solution)/shard_map/all_gather | solution.py:50
  72.4 2.9 %copy.10 = bf16[512,6,2,256]{3,1,2,0:T(8,128)(2,1)S(1)} copy(bf16[512,6,2,256]{3,2,1,0:T(2,128)(2,1)} %all-gather.5.cloned.1.call-done) | data formatting | bytes 6291456 | tf_op jit(solution)/shard_map/all_gather | solution.py:50
  75.3 0.0 copy-start
  75.3 4.4 %convolution_convert_fusion = bf16[4,12,128,2,256]{4,1,3,2,0:T(8,128)(2,1)S(1)} fusion(bf16[4,128,6,2,256]{4,2,3,1,0:T(8,128)(2,1)S(1)} %bitcast.37, s32[4,6]{1,0:T(4,128)S(1)} %bitcast.41, pred[4,6]{1,0:T(4,128)(4,1)S(1)} %iota_compare_fusion.2), kind=kOutput, calls=%fused_computation | convolution fusion | flops 40895040 | bytes 9437304 | tf_op jit(solution)/shard_map/sok,svocx->svkcx/dot_general | solution.py:42
  79.8 0.0 copy-done
  79.8 14.4 %fusion.3 = f32[512,2,2,2,128]{0,4,1,3,2:T(8,128)} fusion(bf16[512,12,2,256,1,1]{3,1,2,0,5,4:T(8,128)(2,1)S(1)} %bitcast.38, bf16[2,128,12,2,256,1]{4,2,3,1,0,5:T(8,128)(2,1)S(1)} %copy-done), kind=kOutput, calls=%fused_computation.5 | convolution fusion | flops 3221225472 | bytes 11534336 | tf_op jit(solution)/shard_map/ikcx,rjkdx->icrdj/dot_general | solution.py:62
  94.2 1.9 %copy.13 = f32[512,2,2,2,128]{4,0,3,2,1:T(8,128)S(1)} copy(f32[512,2,2,2,128]{0,4,1,3,2:T(8,128)} %fusion.3) | data formatting | bytes 4194304 | tf_op jit(solution)/shard_map/ikcx,rjkdx->icrdj/transpose | solution.py:62
  96.1 0.3 copy.14
  96.3 60.3 %all_to_all.5 = f32[32,16,2,2,1,2,128]{6,1,5,3,2,4,0:T(8,128)S(1)} all-to-all(f32[32,16,2,2,1,2,128]{6,1,5,3,2,4,0:T(8,128)S(1)} %copy.14), channel_id=1, replica_groups=mesh['field'=32,'vrow'=2,'vcol'=4] {'field'}, dimensions={0} | all-to-all | bytes 4194304 | tf_op jit(solution)/shard_map/all_to_all | solution.py:29
  156.6 0.1 reduce_sum.9
  156.8 0.7 copy.16
  (1 shorter events, 0.0 us)
Async XLA Ops:
  6.5 20.7 %all-gather.3.cloned.1.call-start = ((), (), s32[]{:S(2)}) async-start(), calls=%async_computation.1 | async-start | bytes 2359296 | tf_op jit(solution)/shard_map/all_gather | solution.py:55
  7.3 65.2 %all-gather.5.cloned.1.call-start = ((), (), s32[]{:S(2)}) async-start(), calls=%async_computation.2 | async-start | bytes 3932160 | tf_op jit(solution)/shard_map/all_gather | solution.py:50
  75.3 4.5 %copy-start = (bf16[2,128,12,2,256,1]{4,2,3,1,0,5:T(8,128)(2,1)S(1)}, bf16[2,128,12,2,256,1]{4,2,3,1,0,5:T(8,128)(2,1)}, u32[]{:S(2)}) copy-start(bf16[2,128,12,2,256,1]{4,2,3,1,0,5:T(8,128)(2,1)} %convert_bitcast_fusion) | copy-start | bytes 9437188
Sparse Core Ops, SparseCore 0:
  9.1 18.0 all-gather.2
  29.1 43.3 all-gather.4
where the time goes:
time: 165 us; the launch traced here: 164 us
  blocking collectives  72.1 us (44%)
  waiting for transfers between devices  47.2 us (29%)
  matrix products  21.9 us (13%)
  between operations  14.1 us (9%)
  local copies, waits for them, and re-layouts  7.99 us (5%)
    all_to_all x1, blocking collectives, sent_and_summed(): parts = lax.all_to_all(split_up(array, dim, length), axis, 0, 0, tiled=True)  60.3 us
    all_gather x1, waiting for transfers between devices, on_device(): lax.all_gather(blocks, 'vcol', axis=0, tiled=True)  40.3 us
    dot_general x1, matrix products, on_device(): jnp.einsum('ikcx,rjkdx->icrdj', rows, columns, preferred_element_type=jnp...  14.4 us
    all_gather x2, blocking collectives, side_by_side(): out = lax.all_gather(both, axis, axis=dim, tiled=True)  11.8 us
    dot_general x2, matrix products, expand(): jnp.einsum('sok,svocx->svkcx', onehot.astype(jnp.bfloat16), shaped, prefe...  7.51 us
    all_gather x1, waiting for transfers between devices, on_device(): lax.all_gather(blocks, 'vrow', axis=0, tiled=True)  5.53 us
  transfers between devices with their start and end apart: 2, of which 2 were waited for; matrix products, arithmetic and copies ran while one was open for 4% of the time, Pallas kernels for 0%

commit v1 on v0

--- a/solution.py
+++ b/solution.py
@@ -6,6 +6,12 @@
 
 SBLK = 12
 BLOCK = 256
+
+
+def gather_from_all(x, axis, dim):
+    size = lax.axis_size(axis)
+    repeats = [size if d == dim else 1 for d in range(x.ndim)]
+    return lax.all_to_all(jnp.tile(x, repeats), axis, split_axis=dim, concat_axis=dim, tiled=True)
 
 
 def side_by_side(arrays, axis, dim, along):
@@ -47,7 +53,7 @@
 
 def on_device(blocks, block_ids, block_counts):
     row_data, row_ids, row_counts = (
-        lax.all_gather(blocks, "vcol", axis=0, tiled=True),
+        gather_from_all(blocks, "vcol", 0),
         *side_by_side((block_ids, block_counts), "vcol", 0, 2),
     )
     rows = expand(row_data, row_ids, row_counts)

time: 165 us -> 151 us (0.915)
  waiting for transfers between devices: 47.2 us -> 0.71 us
  blocking collectives: 72.1 us -> 98.3 us
  starting transfers between devices: 0.04 us -> 4.6 us
  local copies, waits for them, and re-layouts: 7.99 us -> 10.5 us
    all_gather x1 -> x0, waiting for transfers between devices: 40.3 us -> none  [on_device(): lax.all_gather(blocks, 'vcol', axis=0, tiled=True)]
    all_gather x2, blocking collectives: 11.8 us -> 38.2 us  [side_by_side(): out = lax.all_gather(both, axis, axis=dim, tiled=True)]
    all_gather x1, waiting for transfers between devices: 5.53 us -> 0.01 us  [on_device(): lax.all_gather(blocks, 'vrow', axis=0, tiled=True)]
    all_to_all x0 -> x1, starting transfers between devices: none -> 4.59 us  [gather_from_all(): lax.all_to_all(jnp.tile(x, repeats), axis, split_axis=dim, concat_axis=di...]
    another operation x0 -> x1, local copies, waits for them, and re-layouts: none -> 4.43 us  [gather_from_all(): jnp.tile(x, repeats)]
    all_gather x1 -> x0, local copies, waits for them, and re-layouts: 2.87 us -> none  [on_device(): lax.all_gather(blocks, 'vcol', axis=0, tiled=True)]
  transfers between devices with their start and end apart: 2 -> 2, of which waited for: 2 -> 0; matrix products, arithmetic and copies ran while one was open for 4% -> 4% of each run, Pallas kernels for 0% -> 0%
where the time goes in v1:
time: 151 us
  blocking collectives  98.3 us (65%)
  matrix products  21.9 us (15%)
  between operations  14.1 us (9%)
  local copies, waits for them, and re-layouts  10.5 us (7%)
  starting transfers between devices  4.6 us (3%)
    all_to_all x1, blocking collectives, sent_and_summed(): parts = lax.all_to_all(split_up(array, dim, length), axis, 0, 0, tiled=True)  60.1 us
    all_gather x2, blocking collectives, side_by_side(): out = lax.all_gather(both, axis, axis=dim, tiled=True)  38.2 us
    dot_general x1, matrix products, on_device(): jnp.einsum('ikcx,rjkdx->icrdj', rows, columns, preferred_element_type=jnp...  14.4 us
    dot_general x2, matrix products, expand(): jnp.einsum('sok,svocx->svkcx', onehot.astype(jnp.bfloat16), shaped, prefe...  7.5 us
    all_to_all x1, starting transfers between devices, gather_from_all(): lax.all_to_all(jnp.tile(x, repeats), axis, split_axis=dim, concat_axis=di...  4.59 us
    another operation x1, local copies, waits for them, and re-layouts, gather_from_all(): jnp.tile(x, repeats)  4.43 us
  transfers between devices with their start and end apart: 2, of which 0 were waited for; matrix products, arithmetic and copies ran while one was open for 4% of the time, Pallas kernels for 0%

profile of v1, /device:TPU:2, one launch (start us, length us, event | category | flops | bytes accessed | tf_op | source)
XLA Modules:
  0.0 150.6 jit_solution(12868515497530148212)
XLA Ops:
  6.5 4.4 %tile.4 = bf16[4,128,6,2,256]{4,3,2,1,0:T(2,128)(2,1)} broadcast(bf16[128,6,2,256]{3,2,1,0:T(2,128)(2,1)} %param.3), dimensions={1,2,3,4} | broadcast | bytes 3932160 | tf_op jit(solution)/shard_map/tile | solution.py:14
  11.0 0.0 copy-start.1
  11.0 4.6 %all-to-all-start = ((bf16[512,6,2,256]{3,2,1,0:T(2,128)(2,1)}), bf16[512,6,2,256]{3,2,1,0:T(2,128)(2,1)S(1)}, u32[]{:S(2)}, u32[]{:S(2)}) async-start(bf16[512,6,2,256]{3,2,1,0:T(2,128)(2,1)} %bitcast.39), calls=%async_computation | async-start | bytes 6291456 | tf_op jit(solution)/shard_map/all_to_all | solution.py:14
  15.6 0.0 all-gather.2.cloned.1.call-start
  15.6 0.7 all-gather.2.cloned.1.call-update
  16.9 0.0 copy-done.1
  16.9 0.1 pad_add_fusion
  17.0 1.8 %all_gather.9 = s32[2,1,7]{2,1,0:T(1,128)S(1)} all-gather(s32[1,1,7]{2,1,0:T(1,128)S(1)} %pad_add_fusion), channel_id=1, replica_groups=mesh['field'=32,'vrow'=2,'vcol'=4] {'vrow'}, dimensions={0}, use_global_device_ids=true | all-gather | bytes 84 | tf_op jit(solution)/shard_map/all_gather | solution.py:22
  18.8 36.4 %all_gather.11 = s32[4,1,7]{2,1,0:T(1,128)S(1)} all-gather(s32[1,1,7]{2,1,0:T(1,128)S(1)} %pad_add_fusion), channel_id=1, replica_groups=mesh['field'=32,'vrow'=2,'vcol'=4] {'vcol'}, dimensions={0}, use_global_device_ids=true | all-gather | bytes 140 | tf_op jit(solution)/shard_map/all_gather | solution.py:22
  55.2 0.2 slice_reduce_fusion.1
  55.4 0.2 slice_reduce_fusion
  55.7 0.1 iota_compare_fusion.2
  55.8 0.1 iota_compare_fusion.3
  55.8 0.0 all-gather.2.cloned.1.call-done
  55.8 1.9 %copy.9 = bf16[256,6,2,256]{3,1,2,0:T(8,128)(2,1)S(1)} copy(bf16[256,6,2,256]{3,2,1,0:T(2,128)(2,1)} %all-gather.2.cloned.1.call-done) | data formatting | bytes 3145728 | tf_op jit(solution)/shard_map/all_gather | solution.py:61
  57.7 3.1 %convert_bitcast_fusion = bf16[2,128,12,2,256,1]{4,2,3,1,0,5:T(8,128)(2,1)} fusion(bf16[2,128,6,2,256]{4,2,3,1,0:T(8,128)(2,1)S(1)} %bitcast.41, s32[2,6]{1,0:T(2,128)S(1)} %bitcast.44, pred[2,6]{1,0:T(4,128)(4,1)S(1)} %iota_compare_fusion.3), kind=kOutput, calls=%fused_computation.3 | convolution fusion | flops 20447520 | bytes 4718652 | tf_op jit(solution)/shard_map/sok,svocx->svkcx/dot_general | solution.py:48
  60.8 0.0 all-to-all-done
  60.8 1.0 copy.10
  61.8 0.0 copy-start
  61.8 4.4 %convolution_convert_fusion = bf16[4,12,128,2,256]{4,1,3,2,0:T(8,128)(2,1)S(1)} fusion(bf16[4,128,6,2,256]{4,2,3,1,0:T(8,128)(2,1)S(1)} %bitcast.38, s32[4,6]{1,0:T(4,128)S(1)} %bitcast.43, pred[4,6]{1,0:T(4,128)(4,1)S(1)} %iota_compare_fusion.2), kind=kOutput, calls=%fused_computation | convolution fusion | flops 40895040 | bytes 9437304 | tf_op jit(solution)/shard_map/sok,svocx->svkcx/dot_general | solution.py:48
  66.2 0.0 copy-done
  66.2 14.4 %fusion.3 = f32[512,2,2,2,128]{0,4,1,3,2:T(8,128)} fusion(bf16[512,12,2,256,1,1]{3,1,2,0,5,4:T(8,128)(2,1)S(1)} %bitcast.40, bf16[2,128,12,2,256,1]{4,2,3,1,0,5:T(8,128)(2,1)S(1)} %copy-done), kind=kOutput, calls=%fused_computation.5 | convolution fusion | flops 3221225472 | bytes 11534336 | tf_op jit(solution)/shard_map/ikcx,rjkdx->icrdj/dot_general | solution.py:68
  80.6 1.9 %copy.13 = f32[512,2,2,2,128]{4,0,3,2,1:T(8,128)S(1)} copy(f32[512,2,2,2,128]{0,4,1,3,2:T(8,128)} %fusion.3) | data formatting | bytes 4194304 | tf_op jit(solution)/shard_map/ikcx,rjkdx->icrdj/transpose | solution.py:68
  82.5 0.3 copy.14
  82.8 60.1 %all_to_all.10 = f32[32,16,2,2,1,2,128]{6,1,5,3,2,4,0:T(8,128)S(1)} all-to-all(f32[32,16,2,2,1,2,128]{6,1,5,3,2,4,0:T(8,128)S(1)} %copy.14), channel_id=1, replica_groups=mesh['field'=32,'vrow'=2,'vcol'=4] {'field'}, dimensions={0} | all-to-all | bytes 4194304 | tf_op jit(solution)/shard_map/all_to_all | solution.py:35
  142.9 0.1 reduce_sum.9
  143.1 0.7 copy.16
  (1 shorter events, 0.0 us)
Async XLA Ops:
  11.0 6.0 %copy-start.1 = (s32[1,1,6]{2,1,0:T(1,128)S(1)}, s32[1,1,6]{2,1,0:T(1,128)}, u32[]{:S(2)}) copy-start(s32[1,1,6]{2,1,0:T(1,128)} %param.4) | copy-start | bytes 76
  11.0 49.8 %all-to-all-start = ((bf16[512,6,2,256]{3,2,1,0:T(2,128)(2,1)}), bf16[512,6,2,256]{3,2,1,0:T(2,128)(2,1)S(1)}, u32[]{:S(2)}, u32[]{:S(2)}) async-start(bf16[512,6,2,256]{3,2,1,0:T(2,128)(2,1)} %bitcast.39), calls=%async_computation | async-start | bytes 6291456 | tf_op jit(solution)/shard_map/all_to_all | solution.py:14
  15.6 40.3 %all-gather.2.cloned.1.call-start = ((), (), s32[]{:S(2)}) async-start(), calls=%async_computation.2 | async-start | bytes 2359296 | tf_op jit(solution)/shard_map/all_gather | solution.py:61
  61.8 4.5 %copy-start = (bf16[2,128,12,2,256,1]{4,2,3,1,0,5:T(8,128)(2,1)S(1)}, bf16[2,128,12,2,256,1]{4,2,3,1,0,5:T(8,128)(2,1)}, u32[]{:S(2)}) copy-start(bf16[2,128,12,2,256,1]{4,2,3,1,0,5:T(8,128)(2,1)} %convert_bitcast_fusion) | copy-start | bytes 9437188
Sparse Core Ops, SparseCore 0:
  18.2 18.4 all-gather.1
